TPU v7x, 128 devices: a whole 4x4x4 slice. The times are simulated.
128 devices in a mesh: dp: 16 (over y, x_lo, core), shard: 8 (over z, x_hi).
Axes of the slice: x: 4 (x_hi: 2, x_lo: 2; x = x_hi * 2 + x_lo), y: 4, z: 4, core: 2. Of those that a mesh axis runs over, the one named last changes fastest.
Arguments:
- gradients: bfloat16 [16, 88, 512, 512], P('dp', 'shard'), may hold values from -60 to 60
- owners: int32 [8, 11], P('shard'), may hold values from 0 to 15, as said below
- block_param: int32 [88], replicated, may hold values from 0 to 6, never falling along the last dimension, each value on 1 to 25 neighbouring positions
- left_stat: float32 [32, 8, 512, 512], P('dp', 'shard'), may hold values from -4 to 8, as said below
- right_stat: float32 [32, 8, 512, 512], P('dp', 'shard'), may hold values from -4 to 8, as said below
- moment: float32 [32, 8, 512, 512], P('dp', 'shard'), may hold values from 0.5 to 50
- left_root: bfloat16 [32, 8, 512, 512], P('dp', 'shard'), may hold values from -1 to 3.5, as said below
- right_root: bfloat16 [32, 8, 512, 512], P('dp', 'shard'), may hold values from -1 to 3.5, as said below
Outputs:
- new_left: float32 [32, 8, 512, 512], P('dp', 'shard')
- new_right: float32 [32, 8, 512, 512], P('dp', 'shard')
- new_moment: float32 [32, 8, 512, 512], P('dp', 'shard')
- update: bfloat16 [88, 512, 512], P('shard')
Inputs may be any that keep to these rules, and one draw needn't show every extreme that they name: `owners`: in each row, no value occurs more than 2 times, and some value occurs exactly 2 times. `left_stat`: each slot's matrix is symmetric. `right_stat`: each slot's matrix is symmetric. `left_root`: each slot's matrix is symmetric. `right_root`: each slot's matrix is symmetric.
All inputs are finite; a program needn't handle non-finite values.
Results may differ from a plain program's by a relative error of at most 0.0058.
Values may be sent and summed in bfloat16 or wider, within the bound.
A program may use at most 192 MiB of HBM per device.

v0:
```python
import jax
import jax.numpy as jnp
from jax import lax
from jax.sharding import Mesh
from jax.sharding import PartitionSpec as P

NPARAM = 7
DP = ("dp_0", "dp_1", "dp_2")
SHARD = ("shard_0", "shard_1")
DP_SHARD = ("dp_0", "dp_1", "dp_2", "shard_0", "shard_1")
decay_rate = 0.95
tiny_value = 1e-06


def by_axis(x, axes):
    for axis in axes:
        x = lax.psum(x, axis)
    return x


def on_device(gradients, owners, block_param, left_stat, right_stat, moment, left_root, right_root):
    replicas = lax.axis_size(DP)
    capacity = left_stat.shape[0]
    blocks = gradients.shape[1]
    block_width = gradients.shape[3]
    device = lax.axis_index(DP)
    column = lax.axis_index(SHARD)
    owner_row = owners[0]
    counter = jnp.arange(blocks, dtype=jnp.int32)
    same_owner = owner_row[:, None] == owner_row[None, :]
    earlier = counter[None, :] < counter[:, None]
    places = owner_row * capacity + jnp.sum(jnp.where(same_owner & earlier, 1, 0), axis=1).astype(
        jnp.int32
    )
    slot_ids = jnp.arange(replicas * capacity, dtype=jnp.int32)
    matches = places[None, :] == slot_ids[:, None]
    source = jnp.min(jnp.where(matches, counter[None, :], blocks), axis=1)
    partials = gradients[0].astype(jnp.float32)
    row_share = lax.psum_scatter(partials, DP, scatter_dimension=1, tiled=True)
    share_padded = jnp.concatenate(
        [row_share, jnp.zeros((1,) + row_share.shape[1:], jnp.float32)], axis=0
    )
    outgoing = jnp.take(share_padded, source, axis=0).reshape(
        replicas, capacity, block_width // replicas, block_width
    )
    arrived = lax.all_to_all(outgoing, DP, split_axis=0, concat_axis=2, tiled=True)
    summed = arrived[0]
    left_gram = jnp.einsum("cij,ckj->cik", summed, summed, precision=lax.Precision.HIGHEST)
    right_gram = jnp.einsum("cji,cjk->cik", summed, summed, precision=lax.Precision.HIGHEST)
    new_left = decay_rate * left_stat + (1.0 - decay_rate) * left_gram[:, None]
    new_right = decay_rate * right_stat + (1.0 - decay_rate) * right_gram[:, None]
    new_moment = decay_rate * moment + (1.0 - decay_rate) * (summed * summed)[:, None]
    adam_step = summed / (jnp.sqrt(new_moment[:, 0]) + tiny_value)
    left_half = jnp.einsum(
        "cij,cjk->cik",
        left_root[:, 0],
        summed.astype(jnp.bfloat16),
        preferred_element_type=jnp.float32,
    ).astype(jnp.bfloat16)
    direction = jnp.einsum(
        "cij,cjk->cik", left_half, right_root[:, 0], preferred_element_type=jnp.float32
    )
    my_slots = lax.dynamic_slice_in_dim(matches, device * capacity, capacity, 0)
    local_params = lax.dynamic_slice_in_dim(block_param, column * blocks, blocks, 0)
    slot_param = jnp.sum(jnp.where(my_slots, local_params[None, :], 0), axis=1)
    is_live = jnp.any(my_slots, axis=1)
    param_ids = jnp.arange(NPARAM, dtype=jnp.int32)
    member = (slot_param[:, None] == param_ids[None, :]) & is_live[:, None]
    adam_squares = jnp.sum(adam_step * adam_step, axis=(1, 2))
    direction_squares = jnp.sum(direction * direction, axis=(1, 2))
    adam_local = jnp.sum(jnp.where(member, adam_squares[:, None], 0.0), axis=0)
    direction_local = jnp.sum(jnp.where(member, direction_squares[:, None], 0.0), axis=0)
    adam_norm, direction_norm = (by_axis(adam_local, DP_SHARD), by_axis(direction_local, DP_SHARD))
    graft_ratio = jnp.sqrt((adam_norm + tiny_value) / (direction_norm + tiny_value))
    slot_ratio = jnp.sum(jnp.where(member, graft_ratio[None, :], 0.0), axis=1)
    slot_update = (slot_ratio[:, None, None] * direction).astype(jnp.bfloat16)
    returned = lax.all_to_all(slot_update, DP, split_axis=1, concat_axis=0, tiled=True)
    pieces = jnp.take(returned, places, axis=0)
    update = lax.all_gather(pieces, DP, axis=1, tiled=True)
    return (new_left, new_right, new_moment, update)


def solution(mesh):
    finer = Mesh(
        mesh.devices.reshape(4, 2, 2, 4, 2), ("dp_0", "dp_1", "dp_2", "shard_0", "shard_1")
    )
    placed = (
        P(DP, SHARD, None, None),
        P(SHARD, None),
        P(),
        P(DP, SHARD, None, None),
        P(DP, SHARD, None, None),
        P(DP, SHARD, None, None),
        P(DP, SHARD, None, None),
        P(DP, SHARD, None, None),
    )
    return jax.shard_map(
        on_device,
        mesh=finer,
        in_specs=placed,
        out_specs=(
            P(DP, SHARD, None, None),
            P(DP, SHARD, None, None),
            P(DP, SHARD, None, None),
            P(SHARD, None, None),
        ),
        check_vma=False,
    )
```

profile of v0, /device:TPU:1, one launch (start us, length us, event | category | flops | bytes accessed | tf_op | source)
XLA Modules:
  0.0 309.6 jit_solution(17516869295652060086)
XLA Ops:
  7.2 0.0 copy-start
  7.2 0.0 reduce-scatter.2.cloned.1.call-start
  7.2 8.7 %bitcast_convert_fusion = f32[11,512,512]{2,1,0:T(8,128)} fusion(bf16[1,11,512,512]{3,2,1,0:T(8,128)(2,1)} %param.8), kind=kLoop, calls=%fused_computation.2 | loop fusion | flops 2883584 | bytes 17301504 | tf_op jit(solution)/shard_map/convert_element_type | solution.py:38
  15.9 0.0 copy-start.6
  15.9 0.0 reduce-scatter.2.cloned.1.call-update
  15.9 0.6 copy-done.6
  16.6 0.2 select_reduce_fusion.1
  16.7 0.1 select_reduce_fusion
  16.9 0.1 reduce_min.14
  17.0 130.2 %reduce-scatter.2.cloned.1.call-done = f32[11,32,512]{2,1,0:T(8,128)} async-done(((f32[11,512,512]{2,1,0:T(8,128)}), f32[11,32,512]{2,1,0:T(8,128)}) %reduce-scatter.2.cloned.1.call-update) | async-done | bytes 720912 | tf_op jit(solution)/shard_map/reduce_scatter | solution.py:39
  147.2 1.2 concatenate.3
  148.4 2.0 gather_fusion
  150.4 3.1 %broadcast_select_fusion = f32[16,2,32,512]{3,2,1,0:T(8,128)} fusion(f32[16,2,32,512]{3,2,1,0:T(8,128)} %bitcast.83, pred[16,2]{1,0:T(8,128)(4,1)S(1)} %compare_and_fusion), kind=kLoop, calls=%fused_computation.23 | loop fusion | flops 524288 | bytes 4194336 | tf_op jit(solution)/shard_map/jit(_take)/select_n | solution.py:43
  153.5 0.0 copy-start.5
  153.5 5.9 %all-to-all-start = ((f32[16,2,32,512]{3,2,1,0:T(8,128)}), f32[16,2,32,512]{3,2,1,0:T(8,128)S(1)}, u32[]{:S(2)}, u32[]{:S(2)}) async-start(f32[16,2,32,512]{3,2,1,0:T(8,128)} %broadcast_select_fusion), calls=%async_computation.1 | async-start | bytes 4194304 | tf_op jit(solution)/shard_map/all_to_all | solution.py:46
  159.3 0.0 copy-done.5
  159.3 0.1 dynamic_slice.7
  159.4 0.1 fusion.15
  159.5 0.1 select_reduce_fusion.5
  159.7 26.7 %all-to-all-done = f32[16,2,32,512]{3,2,1,0:T(8,128)S(1)} async-done(((f32[16,2,32,512]{3,2,1,0:T(8,128)}), f32[16,2,32,512]{3,2,1,0:T(8,128)S(1)}, u32[]{:S(2)}, u32[]{:S(2)}) %all-to-all-start) | async-done | bytes 2097184 | tf_op jit(solution)/shard_map/all_to_all | solution.py:46
  186.4 0.0 copy-start.2
  186.4 0.3 multiply_multiply_fusion
  186.6 1.1 copy-done.2
  187.7 0.2 copy.65
  187.9 0.0 copy-start.3
  188.0 2.0 copy.61
  189.9 0.3 copy-done.3
  190.2 2.8 sqrt_add_fusion
  192.9 0.0 copy-done
  193.0 4.0 %multiply_reduce_fusion = (f32[2]{0:T(128)S(1)}, f32[2,512,512]{2,1,0:T(8,128)}) fusion(bf16[2,1,512,512]{3,2,1,0:T(8,128)(2,1)S(1)} %copy-done, bf16[2,1,512,512]{3,2,1,0:T(8,128)(2,1)} %param.14, f32[2,512,512]{2,1,0:T(8,128)S(1)} %bitcast.79), kind=kOutput, calls=%fused_computation.14 | convolution fusion | flops 1075838976 | bytes 6291464 | tf_op jit(solution)/shard_map/cij,cjk->cik/dot_general | solution.py:60
  197.0 2.7 fusion.3
  199.6 0.1 select_reduce_fusion.4
  199.7 7.2 %all-reduce.2 = (f32[7]{0:T(128)S(1)}, f32[7]{0:T(128)S(1)}) all-reduce(f32[7]{0:T(128)S(1)} %get-tuple-element.25, f32[7]{0:T(128)S(1)} %get-tuple-element.24), channel_id=1, replica_groups=mesh['dp_0'=4,'dp_1'=2,'dp_2'=2,'shard_0'=4,'shard_1'=2] {'dp_0'}, use_global_device_ids=true, to_apply=%region_14.15 | all-reduce | flops 14 | bytes 112 | tf_op jit(solution)/shard_map/psum | solution.py:17
  206.9 3.8 %all-reduce.5 = (f32[7]{0:T(128)S(1)}, f32[7]{0:T(128)S(1)}) all-reduce(f32[7]{0:T(128)S(1)} %get-tuple-element.28, f32[7]{0:T(128)S(1)} %get-tuple-element.29), channel_id=1, replica_groups=mesh['dp_0'=4,'dp_1'=2,'dp_2'=2,'shard_0'=4,'shard_1'=2] {'dp_1'}, use_global_device_ids=true, to_apply=%region_15.16 | all-reduce | flops 14 | bytes 112 | tf_op jit(solution)/shard_map/psum | solution.py:17
  210.7 6.2 %all-reduce.4 = (f32[7]{0:T(128)S(1)}, f32[7]{0:T(128)S(1)}) all-reduce(f32[7]{0:T(128)S(1)} %get-tuple-element.34, f32[7]{0:T(128)S(1)} %get-tuple-element.35), channel_id=1, replica_groups=mesh['dp_0'=4,'dp_1'=2,'dp_2'=2,'shard_0'=4,'shard_1'=2] {'dp_2'}, use_global_device_ids=true, to_apply=%region_16.17 | all-reduce | flops 14 | bytes 112 | tf_op jit(solution)/shard_map/psum | solution.py:17
  216.9 8.7 %all-reduce.1 = (f32[7]{0:T(128)S(1)}, f32[7]{0:T(128)S(1)}) all-reduce(f32[7]{0:T(128)S(1)} %get-tuple-element.32, f32[7]{0:T(128)S(1)} %get-tuple-element.33), channel_id=1, replica_groups=mesh['dp_0'=4,'dp_1'=2,'dp_2'=2,'shard_0'=4,'shard_1'=2] {'shard_0'}, use_global_device_ids=true, to_apply=%region_17.18 | all-reduce | flops 14 | bytes 112 | tf_op jit(solution)/shard_map/psum | solution.py:17
  225.6 5.3 %all-reduce.3 = (f32[7]{0:T(128)S(1)}, f32[7]{0:T(128)S(1)}) all-reduce(f32[7]{0:T(128)S(1)} %get-tuple-element.26, f32[7]{0:T(128)S(1)} %get-tuple-element.27), channel_id=1, replica_groups=mesh['dp_0'=4,'dp_1'=2,'dp_2'=2,'shard_0'=4,'shard_1'=2] {'shard_1'}, use_global_device_ids=true, to_apply=%region_18.19 | all-reduce | flops 14 | bytes 112 | tf_op jit(solution)/shard_map/psum | solution.py:17
  230.9 0.2 select_reduce_fusion.2
  231.1 1.9 multiply_convert_fusion
  233.0 2.0 copy.69
  235.0 7.0 %all-to-all-start.1 = ((bf16[2,512,512]{2,0,1:T(2,128)(2,1)}), bf16[2,512,512]{2,0,1:T(2,128)(2,1)S(1)}, u32[]{:S(2)}, u32[]{:S(2)}) async-start(bf16[2,512,512]{2,0,1:T(2,128)(2,1)} %copy.69), calls=%async_computation.2 | async-start | bytes 2097152 | tf_op jit(solution)/shard_map/all_to_all | solution.py:77
  242.0 0.2 all-gather.2.cloned.1.call-start
  242.2 15.5 %all-to-all-done.1 = bf16[2,512,512]{2,0,1:T(2,128)(2,1)S(1)} async-done(((bf16[2,512,512]{2,0,1:T(2,128)(2,1)}), bf16[2,512,512]{2,0,1:T(2,128)(2,1)S(1)}, u32[]{:S(2)}, u32[]{:S(2)}) %all-to-all-start.1) | async-done | bytes 1048608 | tf_op jit(solution)/shard_map/all_to_all | solution.py:77
  257.7 0.2 copy.70
  257.9 0.1 copy.71
  258.0 0.6 gather_fusion.1
  258.6 0.8 broadcast_select_fusion.1
  259.4 0.0 all-gather.2.cloned.1.call-update
  259.4 0.0 copy-start.4
  259.4 6.1 %fusion = f32[2,1,512,512]{3,2,1,0:T(8,128)} fusion(f32[2,1,512,512]{3,2,1,0:T(8,128)} %param.12, f32[2,512,512]{2,1,0:T(8,128)S(1)} %bitcast.80), kind=kOutput, calls=%fused_computation.6 | convolution fusion | flops 3222798336 | bytes 6291456 | tf_op jit(solution)/shard_map/cji,cjk->cik/dot_general | solution.py:49
  265.6 0.0 copy-done.4
  265.6 5.0 %fusion.1 = f32[2,1,512,512]{3,2,1,0:T(8,128)} fusion(f32[2,1,512,512]{3,2,1,0:T(8,128)S(1)} %copy-done.4, f32[2,512,512]{2,1,0:T(8,128)S(1)} %bitcast.81), kind=kOutput, calls=%fused_computation.9 | convolution fusion | flops 3222798336 | bytes 6291456 | tf_op jit(solution)/shard_map/cij,ckj->cik/dot_general | solution.py:48
  270.6 26.5 %all-gather.2.cloned.1.call-done = bf16[11,512,512]{2,1,0:T(8,128)(2,1)} async-done(((bf16[11,32,512]{2,1,0:T(8,128)(2,1)}), bf16[11,512,512]{2,1,0:T(8,128)(2,1)}) %all-gather.2.cloned.1.call-update) | async-done | bytes 5767184 | tf_op jit(solution)/shard_map/all_gather | solution.py:79
  297.1 0.0 copy-start.1
  297.1 5.6 %copy.85 = bf16[11,512,512]{2,1,0:T(8,128)(2,1)} copy(bf16[11,512,512]{2,1,0:T(8,128)(2,1)} %all-gather.2.cloned.1.call-done) | data formatting | bytes 11534336
  302.7 0.0 copy-done.1
  (9 shorter events, 0.1 us)
Async XLA Ops:
  7.2 185.8 %copy-start = (bf16[2,1,512,512]{3,2,1,0:T(8,128)(2,1)S(1)}, bf16[2,1,512,512]{3,2,1,0:T(8,128)(2,1)}, u32[]{:S(2)}) copy-start(bf16[2,1,512,512]{3,2,1,0:T(8,128)(2,1)} %param.15) | copy-start | bytes 3145732
  7.2 140.0 %reduce-scatter.2.cloned.1.call-start = ((), (), s32[]{:S(2)}) async-start(), calls=%async_computation.3 | async-start | bytes 12255232 | tf_op jit(solution)/shard_map/reduce_scatter | solution.py:39
  15.9 0.7 copy-start.6
  153.5 5.9 %copy-start.5 = (s32[88]{0:T(128)S(1)}, s32[88]{0:T(128)}, u32[]{:S(2)}) copy-start(s32[88]{0:T(128)} %param.10) | copy-start | bytes 1060
  153.5 32.9 %all-to-all-start = ((f32[16,2,32,512]{3,2,1,0:T(8,128)}), f32[16,2,32,512]{3,2,1,0:T(8,128)S(1)}, u32[]{:S(2)}, u32[]{:S(2)}) async-start(f32[16,2,32,512]{3,2,1,0:T(8,128)} %broadcast_select_fusion), calls=%async_computation.1 | async-start | bytes 4194304 | tf_op jit(solution)/shard_map/all_to_all | solution.py:46
  186.4 1.3 copy-start.2
  187.9 2.2 copy-start.3
  235.0 22.7 %all-to-all-start.1 = ((bf16[2,512,512]{2,0,1:T(2,128)(2,1)}), bf16[2,512,512]{2,0,1:T(2,128)(2,1)S(1)}, u32[]{:S(2)}, u32[]{:S(2)}) async-start(bf16[2,512,512]{2,0,1:T(2,128)(2,1)} %copy.69), calls=%async_computation.2 | async-start | bytes 2097152 | tf_op jit(solution)/shard_map/all_to_all | solution.py:77
  242.0 55.1 %all-gather.2.cloned.1.call-start = ((), (), s32[]{:S(2)}) async-start(), calls=%async_computation.4 | async-start | bytes 6127616 | tf_op jit(solution)/shard_map/all_gather | solution.py:79
  259.4 6.2 %copy-start.4 = (f32[2,1,512,512]{3,2,1,0:T(8,128)S(1)}, f32[2,1,512,512]{3,2,1,0:T(8,128)}, u32[]{:S(2)}) copy-start(f32[2,1,512,512]{3,2,1,0:T(8,128)} %param.11) | copy-start | bytes 6291460
  297.1 5.6 %copy-start.1 = (bf16[2,1,512,512]{3,2,1,0:T(8,128)(2,1)S(1)}, bf16[2,1,512,512]{3,2,1,0:T(8,128)(2,1)}, u32[]{:S(2)}) copy-start(bf16[2,1,512,512]{3,2,1,0:T(8,128)(2,1)} %param.15) | copy-start | bytes 3145732
Sparse Core Ops, SparseCore 0:
  16.0 131.0 reduce-scatter.1
  259.6 37.5 all-gather.1
where the time goes:
time: 310 us
  waiting for transfers between devices  199 us (64%)
  blocking collectives  31.1 us (10%)
  other arithmetic  21.1 us (7%)
  local copies, waits for them, and re-layouts  16 us (5%)
  matrix products  15.1 us (5%)
  between operations  14.2 us (5%)
  starting transfers between devices  13.1 us (4%)
    reduce_scatter x1, waiting for transfers between devices, on_device(): row_share = lax.psum_scatter(partials, DP, scatter_dimension=1, tiled=True)  130 us
    psum x5, blocking collectives, by_axis(): x = lax.psum(x, axis)  31.1 us
    all_to_all x1, waiting for transfers between devices, on_device(): lax.all_to_all(outgoing, DP, split_axis=0, concat_axis=2, tiled=True)  26.7 us
    all_gather x1, waiting for transfers between devices, on_device(): update = lax.all_gather(pieces, DP, axis=1, tiled=True)  26.5 us
    all_to_all x1, waiting for transfers between devices, on_device(): lax.all_to_all(slot_update, DP, split_axis=1, concat_axis=0, tiled=True)  15.5 us
    convert_element_type x1, other arithmetic, on_device(): partials = gradients[0].astype(jnp.float32)  8.67 us
    unnamed x15, local copies, waits for them, and re-layouts  7.59 us
    all_to_all x1, starting transfers between devices, on_device(): lax.all_to_all(slot_update, DP, split_axis=1, concat_axis=0, tiled=True)  6.96 us
  transfers between devices with their start and end apart: 4, of which 4 were waited for; matrix products, arithmetic and copies ran while one was open for 4% of the time, Pallas kernels for 0%

commit v1 on v0

--- a/solution.py
+++ b/solution.py
@@ -43,7 +43,9 @@
     outgoing = jnp.take(share_padded, source, axis=0).reshape(
         replicas, capacity, block_width // replicas, block_width
     )
-    arrived = lax.all_to_all(outgoing, DP, split_axis=0, concat_axis=2, tiled=True)
+    parts = jnp.split(outgoing, lax.axis_size(DP), axis=0)
+    arrived_2 = lax.all_to_all(jnp.stack(parts), DP, 0, 0)
+    arrived = jnp.concatenate(arrived_2, axis=2)
     summed = arrived[0]
     left_gram = jnp.einsum("cij,ckj->cik", summed, summed, precision=lax.Precision.HIGHEST)
     right_gram = jnp.einsum("cji,cjk->cik", summed, summed, precision=lax.Precision.HIGHEST)

time: 310 us -> 319 us (1.029)
  local copies, waits for them, and re-layouts: 16 us -> 26.5 us
    unnamed x15 -> x30, local copies, waits for them, and re-layouts: 7.59 us -> 17.5 us
where the time goes in v1:
time: 319 us
  waiting for transfers between devices  199 us (62%)
  blocking collectives  31.1 us (10%)
  local copies, waits for them, and re-layouts  26.5 us (8%)
  other arithmetic  19.8 us (6%)
  matrix products  15.1 us (5%)
  between operations  14.2 us (4%)
  starting transfers between devices  13.1 us (4%)
    reduce_scatter x1, waiting for transfers between devices, on_device(): row_share = lax.psum_scatter(partials, DP, scatter_dimension=1, tiled=True)  130 us
    psum x5, blocking collectives, by_axis(): x = lax.psum(x, axis)  31.1 us
    all_to_all x1, waiting for transfers between devices, on_device(): arrived_2 = lax.all_to_all(jnp.stack(parts), DP, 0, 0)  26.7 us
    all_gather x1, waiting for transfers between devices, on_device(): update = lax.all_gather(pieces, DP, axis=1, tiled=True)  26.5 us
    unnamed x30, local copies, waits for them, and re-layouts  17.5 us
    all_to_all x1, waiting for transfers between devices, on_device(): lax.all_to_all(slot_update, DP, split_axis=1, concat_axis=0, tiled=True)  15.5 us
    convert_element_type x1, other arithmetic, on_device(): partials = gradients[0].astype(jnp.float32)  8.67 us
    all_to_all x1, starting transfers between devices, on_device(): lax.all_to_all(slot_update, DP, split_axis=1, concat_axis=0, tiled=True)  6.96 us
  transfers between devices with their start and end apart: 4, of which 4 were waited for; matrix products, arithmetic and copies ran while one was open for 4% of the time, Pallas kernels for 0%

profile of v1, /device:TPU:1, one launch (start us, length us, event | category | flops | bytes accessed | tf_op | source)
XLA Modules:
  0.0 318.9 jit_solution(14419111593601905721)
XLA Ops:
  7.2 0.0 copy-start
  7.2 0.0 reduce-scatter.2.cloned.1.call-start
  7.2 8.7 %bitcast_convert_fusion = f32[11,512,512]{2,1,0:T(8,128)} fusion(bf16[1,11,512,512]{3,2,1,0:T(8,128)(2,1)} %param.8), kind=kLoop, calls=%fused_computation.2 | loop fusion | flops 2883584 | bytes 17301504 | tf_op jit(solution)/shard_map/convert_element_type | solution.py:38
  15.9 0.0 reduce-scatter.2.cloned.1.call-update
  15.9 0.6 copy-done.6
  16.6 0.2 select_reduce_fusion.1
  16.7 0.1 select_reduce_fusion
  16.9 130.3 %reduce-scatter.2.cloned.1.call-done = f32[11,32,512]{2,1,0:T(8,128)} async-done(((f32[11,512,512]{2,1,0:T(8,128)}), f32[11,32,512]{2,1,0:T(8,128)}) %reduce-scatter.2.cloned.1.call-update) | async-done | bytes 720912 | tf_op jit(solution)/shard_map/reduce_scatter | solution.py:39
  147.2 1.2 concatenate.3
  148.4 2.0 gather_fusion
  150.4 1.8 broadcast_select_fusion
  152.2 0.7 fusion.25
  152.8 0.7 fusion.24
  153.5 0.7 fusion.23
  154.2 0.7 fusion.22
  154.8 0.7 fusion.21
  155.5 0.7 fusion.20
  156.1 0.7 fusion.19
  156.8 0.7 fusion.18
  157.5 0.7 fusion.17
  158.1 0.7 fusion.16
  158.8 0.7 fusion.15
  159.5 0.7 fusion.14
  160.1 0.7 fusion.13
  160.8 0.7 fusion.12
  161.5 0.7 fusion.11
  162.1 0.7 fusion.10
  162.8 5.9 %all-to-all-start = ((f32[16,1,2,32,512]{4,3,2,1,0:T(8,128)}), f32[16,1,2,32,512]{4,3,2,1,0:T(8,128)S(1)}, u32[]{:S(2)}, u32[]{:S(2)}) async-start(f32[16,1,2,32,512]{4,3,2,1,0:T(8,128)} %fusion.10), calls=%async_computation.1 | async-start | bytes 4194304 | tf_op jit(solution)/shard_map/all_to_all | solution.py:47
  168.6 0.0 copy-done.5
  168.7 0.1 dynamic_slice.7
  168.7 0.1 fusion.31
  168.9 0.1 select_reduce_fusion.5
  169.0 26.7 %all-to-all-done = f32[16,1,2,32,512]{4,3,2,1,0:T(8,128)S(1)} async-done(((f32[16,1,2,32,512]{4,3,2,1,0:T(8,128)}), f32[16,1,2,32,512]{4,3,2,1,0:T(8,128)S(1)}, u32[]{:S(2)}, u32[]{:S(2)}) %all-to-all-start) | async-done | bytes 2097184 | tf_op jit(solution)/shard_map/all_to_all | solution.py:47
  195.7 0.3 multiply_multiply_fusion
  196.0 1.1 copy-done.2
  197.0 0.2 copy.67
  197.3 0.0 copy-start.3
  197.3 2.0 copy.63
  199.2 0.3 copy-done.3
  199.5 2.8 sqrt_add_fusion
  202.3 4.0 %multiply_reduce_fusion = (f32[2]{0:T(128)S(1)}, f32[2,512,512]{2,1,0:T(8,128)}) fusion(bf16[2,1,512,512]{3,2,1,0:T(8,128)(2,1)S(1)} %copy-done, bf16[2,1,512,512]{3,2,1,0:T(8,128)(2,1)} %param.14, f32[2,512,512]{2,1,0:T(8,128)S(1)} %bitcast.140), kind=kOutput, calls=%fused_computation.14 | convolution fusion | flops 1075838976 | bytes 6291464 | tf_op jit(solution)/shard_map/cij,cjk->cik/dot_general | solution.py:62
  206.3 2.7 fusion.3
  208.9 0.1 select_reduce_fusion.4
  209.0 7.2 %all-reduce.2 = (f32[7]{0:T(128)S(1)}, f32[7]{0:T(128)S(1)}) all-reduce(f32[7]{0:T(128)S(1)} %get-tuple-element.25, f32[7]{0:T(128)S(1)} %get-tuple-element.24), channel_id=1, replica_groups=mesh['dp_0'=4,'dp_1'=2,'dp_2'=2,'shard_0'=4,'shard_1'=2] {'dp_0'}, use_global_device_ids=true, to_apply=%region_14.15 | all-reduce | flops 14 | bytes 112 | tf_op jit(solution)/shard_map/psum | solution.py:17
  216.2 3.8 %all-reduce.5 = (f32[7]{0:T(128)S(1)}, f32[7]{0:T(128)S(1)}) all-reduce(f32[7]{0:T(128)S(1)} %get-tuple-element.28, f32[7]{0:T(128)S(1)} %get-tuple-element.29), channel_id=1, replica_groups=mesh['dp_0'=4,'dp_1'=2,'dp_2'=2,'shard_0'=4,'shard_1'=2] {'dp_1'}, use_global_device_ids=true, to_apply=%region_15.16 | all-reduce | flops 14 | bytes 112 | tf_op jit(solution)/shard_map/psum | solution.py:17
  220.0 6.2 %all-reduce.4 = (f32[7]{0:T(128)S(1)}, f32[7]{0:T(128)S(1)}) all-reduce(f32[7]{0:T(128)S(1)} %get-tuple-element.34, f32[7]{0:T(128)S(1)} %get-tuple-element.35), channel_id=1, replica_groups=mesh['dp_0'=4,'dp_1'=2,'dp_2'=2,'shard_0'=4,'shard_1'=2] {'dp_2'}, use_global_device_ids=true, to_apply=%region_16.17 | all-reduce | flops 14 | bytes 112 | tf_op jit(solution)/shard_map/psum | solution.py:17
  226.2 8.7 %all-reduce.1 = (f32[7]{0:T(128)S(1)}, f32[7]{0:T(128)S(1)}) all-reduce(f32[7]{0:T(128)S(1)} %get-tuple-element.32, f32[7]{0:T(128)S(1)} %get-tuple-element.33), channel_id=1, replica_groups=mesh['dp_0'=4,'dp_1'=2,'dp_2'=2,'shard_0'=4,'shard_1'=2] {'shard_0'}, use_global_device_ids=true, to_apply=%region_17.18 | all-reduce | flops 14 | bytes 112 | tf_op jit(solution)/shard_map/psum | solution.py:17
  234.9 5.3 %all-reduce.3 = (f32[7]{0:T(128)S(1)}, f32[7]{0:T(128)S(1)}) all-reduce(f32[7]{0:T(128)S(1)} %get-tuple-element.26, f32[7]{0:T(128)S(1)} %get-tuple-element.27), channel_id=1, replica_groups=mesh['dp_0'=4,'dp_1'=2,'dp_2'=2,'shard_0'=4,'shard_1'=2] {'shard_1'}, use_global_device_ids=true, to_apply=%region_18.19 | all-reduce | flops 14 | bytes 112 | tf_op jit(solution)/shard_map/psum | solution.py:17
  240.2 0.2 select_reduce_fusion.2
  240.4 1.9 multiply_convert_fusion
  242.3 2.0 copy.71
  244.3 7.0 %all-to-all-start.1 = ((bf16[2,512,512]{2,0,1:T(2,128)(2,1)}), bf16[2,512,512]{2,0,1:T(2,128)(2,1)S(1)}, u32[]{:S(2)}, u32[]{:S(2)}) async-start(bf16[2,512,512]{2,0,1:T(2,128)(2,1)} %copy.71), calls=%async_computation.2 | async-start | bytes 2097152 | tf_op jit(solution)/shard_map/all_to_all | solution.py:79
  251.3 0.2 all-gather.2.cloned.1.call-start
  251.6 15.5 %all-to-all-done.1 = bf16[2,512,512]{2,0,1:T(2,128)(2,1)S(1)} async-done(((bf16[2,512,512]{2,0,1:T(2,128)(2,1)}), bf16[2,512,512]{2,0,1:T(2,128)(2,1)S(1)}, u32[]{:S(2)}, u32[]{:S(2)}) %all-to-all-start.1) | async-done | bytes 1048608 | tf_op jit(solution)/shard_map/all_to_all | solution.py:79
  267.1 0.2 copy.72
  267.2 0.1 copy.73
  267.3 0.6 gather_fusion.1
  267.9 0.8 broadcast_select_fusion.1
  268.7 0.0 all-gather.2.cloned.1.call-update
  268.7 0.0 copy-start.4
  268.8 6.1 %fusion = f32[2,1,512,512]{3,2,1,0:T(8,128)} fusion(f32[2,1,512,512]{3,2,1,0:T(8,128)} %param.12, f32[2,512,512]{2,1,0:T(8,128)S(1)} %bitcast.141), kind=kOutput, calls=%fused_computation.6 | convolution fusion | flops 3222798336 | bytes 6291456 | tf_op jit(solution)/shard_map/cji,cjk->cik/dot_general | solution.py:51
  274.9 5.0 %fusion.1 = f32[2,1,512,512]{3,2,1,0:T(8,128)} fusion(f32[2,1,512,512]{3,2,1,0:T(8,128)S(1)} %copy-done.4, f32[2,512,512]{2,1,0:T(8,128)S(1)} %bitcast.142), kind=kOutput, calls=%fused_computation.9 | convolution fusion | flops 3222798336 | bytes 6291456 | tf_op jit(solution)/shard_map/cij,ckj->cik/dot_general | solution.py:50
  279.9 26.5 %all-gather.2.cloned.1.call-done = bf16[11,512,512]{2,1,0:T(8,128)(2,1)} async-done(((bf16[11,32,512]{2,1,0:T(8,128)(2,1)}), bf16[11,512,512]{2,1,0:T(8,128)(2,1)}) %all-gather.2.cloned.1.call-update) | async-done | bytes 5767184 | tf_op jit(solution)/shard_map/all_gather | solution.py:81
  306.4 5.6 %copy.102 = bf16[11,512,512]{2,1,0:T(8,128)(2,1)} copy(bf16[11,512,512]{2,1,0:T(8,128)(2,1)} %all-gather.2.cloned.1.call-done) | data formatting | bytes 11534336
  (16 shorter events, 0.1 us)
Async XLA Ops:
  7.2 195.1 %copy-start = (bf16[2,1,512,512]{3,2,1,0:T(8,128)(2,1)S(1)}, bf16[2,1,512,512]{3,2,1,0:T(8,128)(2,1)}, u32[]{:S(2)}) copy-start(bf16[2,1,512,512]{3,2,1,0:T(8,128)(2,1)} %param.15) | copy-start | bytes 3145732
  7.2 140.0 %reduce-scatter.2.cloned.1.call-start = ((), (), s32[]{:S(2)}) async-start(), calls=%async_computation.3 | async-start | bytes 12255232 | tf_op jit(solution)/shard_map/reduce_scatter | solution.py:39
  15.9 0.7 copy-start.6
  162.8 5.9 %copy-start.5 = (s32[88]{0:T(128)S(1)}, s32[88]{0:T(128)}, u32[]{:S(2)}) copy-start(s32[88]{0:T(128)} %param.10) | copy-start | bytes 1060
  162.8 32.9 %all-to-all-start = ((f32[16,1,2,32,512]{4,3,2,1,0:T(8,128)}), f32[16,1,2,32,512]{4,3,2,1,0:T(8,128)S(1)}, u32[]{:S(2)}, u32[]{:S(2)}) async-start(f32[16,1,2,32,512]{4,3,2,1,0:T(8,128)} %fusion.10), calls=%async_computation.1 | async-start | bytes 4194304 | tf_op jit(solution)/shard_map/all_to_all | solution.py:47
  195.7 1.3 copy-start.2
  197.3 2.2 copy-start.3
  244.3 22.7 %all-to-all-start.1 = ((bf16[2,512,512]{2,0,1:T(2,128)(2,1)}), bf16[2,512,512]{2,0,1:T(2,128)(2,1)S(1)}, u32[]{:S(2)}, u32[]{:S(2)}) async-start(bf16[2,512,512]{2,0,1:T(2,128)(2,1)} %copy.71), calls=%async_computation.2 | async-start | bytes 2097152 | tf_op jit(solution)/shard_map/all_to_all | solution.py:79
  251.3 55.1 %all-gather.2.cloned.1.call-start = ((), (), s32[]{:S(2)}) async-start(), calls=%async_computation.4 | async-start | bytes 6127616 | tf_op jit(solution)/shard_map/all_gather | solution.py:81
  268.7 6.2 %copy-start.4 = (f32[2,1,512,512]{3,2,1,0:T(8,128)S(1)}, f32[2,1,512,512]{3,2,1,0:T(8,128)}, u32[]{:S(2)}) copy-start(f32[2,1,512,512]{3,2,1,0:T(8,128)} %param.11) | copy-start | bytes 6291460
  306.4 5.6 %copy-start.1 = (bf16[2,1,512,512]{3,2,1,0:T(8,128)(2,1)S(1)}, bf16[2,1,512,512]{3,2,1,0:T(8,128)(2,1)}, u32[]{:S(2)}) copy-start(bf16[2,1,512,512]{3,2,1,0:T(8,128)(2,1)} %param.15) | copy-start | bytes 3145732
Sparse Core Ops, SparseCore 0:
  16.0 131.0 reduce-scatter.1
  268.9 37.5 all-gather.1
